TPU v7x, 32 devices: a whole 2x2x4 slice. The times are simulated.
32 devices in a mesh: wave: 16 (over z, x, core), lev: 2 (over y).
Axes of the slice: x: 2, y: 2, z: 4, core: 2. Of those that a mesh axis runs over, the one named last changes fastest.
Arguments:
- spin_tendency: bfloat16 [32, 2, 136, 768], P('wave', None, 'lev'), may hold values from -6 to 6
- spreading_source: bfloat16 [32, 2, 136, 768], P('wave', None, 'lev'), may hold values from -6 to 6
- heat_source: bfloat16 [32, 2, 136, 768], P('wave', None, 'lev'), may hold values from -6 to 6
- helmholtz_inverses: bfloat16 [2, 384, 136, 136], P('lev', 'wave'), may hold values from -0.5 to 0.5
- heat_spreading_coupler: bfloat16 [136, 136], replicated, may hold values from -0.5 to 0.5
- smoothing_strengths: float32 [136], replicated, may hold values from 0.5 to 30
- azimuthal_order_list: int32 [32], P('wave'), may hold values from 0 to 767
Outputs:
- vorticity_new: bfloat16 [32, 2, 136, 768], P('wave', None, 'lev')
- divergence_new: bfloat16 [32, 2, 136, 768], P('wave', None, 'lev')
- temperature_new: bfloat16 [32, 2, 136, 768], P('wave', None, 'lev')
All inputs are finite; a program needn't handle non-finite values.
Results may differ from a plain program's by a relative error of at most 0.0075.
Values may be sent and summed in bfloat16 or wider, within the bound.
A program may use at most 64 MiB of HBM per device.

v0:
```python
import jax
import jax.numpy as jnp
from jax import lax
from jax.sharding import PartitionSpec as P


def damping_table(level_gain, wavenumbers, total_n):
    scaled = (wavenumbers * (wavenumbers + 1)).astype(jnp.float32) / jnp.float32(
        (total_n - 1) * total_n
    )
    return 1.0 / (1.0 + level_gain[:, None] * scaled[None, :] ** 2)


def on_device(
    spin_tendency,
    spreading_source,
    heat_source,
    helmholtz_inverses,
    heat_spreading_coupler,
    smoothing_strengths,
    azimuthal_order_list,
):
    lev_count = lax.axis_size("lev")
    lev_index = lax.axis_index("lev")
    row_count, part_count, lev_local, total_n = spreading_source.shape
    block_n = total_n // lev_count
    layer_count = lev_local * lev_count
    flat_rows = row_count * part_count
    empty_placeholder = jnp.zeros((), jnp.bfloat16)
    wave_count = lax.axis_size("wave")
    local_n = block_n // wave_count
    rhs_div = lax.all_to_all(spreading_source, "lev", split_axis=3, concat_axis=2, tiled=True)
    outgoing = rhs_div.reshape(flat_rows, layer_count, wave_count, local_n).transpose(2, 3, 0, 1)
    outgoing = outgoing.reshape(wave_count, local_n, flat_rows * layer_count)
    columns = lax.all_to_all(outgoing, "wave", split_axis=0, concat_axis=0, tiled=True)
    columns = columns.reshape(wave_count, local_n, flat_rows, layer_count)
    solved_columns = jnp.einsum(
        "jkp,wjcp->wjck", helmholtz_inverses[0], columns, preferred_element_type=jnp.float32
    ).astype(jnp.bfloat16)
    solved_columns = solved_columns.reshape(wave_count, local_n, flat_rows * layer_count)
    returned = lax.all_to_all(solved_columns, "wave", split_axis=0, concat_axis=0, tiled=True)
    answer_fields = returned.reshape(block_n, flat_rows, layer_count).transpose(1, 2, 0)
    coupled = jnp.einsum(
        "om,dms->dos", heat_spreading_coupler, answer_fields, preferred_element_type=jnp.float32
    ).astype(jnp.bfloat16)
    both = jnp.stack([answer_fields, coupled])
    both = lax.all_to_all(both, "lev", split_axis=2, concat_axis=3, tiled=True)
    both = both.reshape(2, row_count, part_count, lev_local, total_n)
    spreading_updated, coupled_out = (both[0], both[1])
    heat_updated = (heat_source.astype(jnp.float32) - coupled_out.astype(jnp.float32)).astype(
        jnp.bfloat16
    )
    level_gain = lax.dynamic_slice_in_dim(smoothing_strengths, lev_index * lev_local, lev_local)
    damping = damping_table(level_gain, jnp.arange(total_n, dtype=jnp.int32), total_n)
    spin_updated = (spin_tendency.astype(jnp.float32) * damping[None, None]).astype(jnp.bfloat16)
    interior_slice = (
        jnp.arange(total_n, dtype=jnp.int32)[None, :] >= azimuthal_order_list[:, None]
    )[:, None, None, :]
    return (
        jnp.where(interior_slice, spin_updated, empty_placeholder),
        jnp.where(interior_slice, spreading_updated, empty_placeholder),
        jnp.where(interior_slice, heat_updated, empty_placeholder),
    )


def solution(mesh):
    return jax.shard_map(
        on_device,
        mesh=mesh,
        in_specs=(
            P("wave", None, "lev", None),
            P("wave", None, "lev", None),
            P("wave", None, "lev", None),
            P("lev", "wave", None, None),
            P(),
            P(),
            P("wave"),
        ),
        out_specs=(
            P("wave", None, "lev", None),
            P("wave", None, "lev", None),
            P("wave", None, "lev", None),
        ),
        check_vma=False,
    )
```

profile of v0, /device:TPU:0, one launch (start us, length us, event | category | flops | bytes accessed | tf_op | source)
XLA Modules:
  0.0 88.3 jit_solution(10291500777090711552)
XLA Ops:
  0.6 2.8 %copy.51 = bf16[2,2,68,768]{2,1,0,3:T(2,128)(2,1)S(1)} copy(bf16[2,2,68,768]{3,1,2,0:T(2,128)(2,1)} %param.8) | data formatting | bytes 835584 | tf_op args[1]
  3.5 14.8 %all_to_all.40 = bf16[2,2,68,768]{2,1,0,3:T(2,128)(2,1)S(1)} all-to-all(bf16[2,2,68,768]{2,1,0,3:T(2,128)(2,1)S(1)} %copy.51), channel_id=1, replica_groups=mesh['wave'=16,'lev'=2] {'lev'}, dimensions={3} | all-to-all | bytes 835584 | tf_op jit(solution)/shard_map/all_to_all | solution.py:32
  18.3 0.8 copy.71
  19.2 0.4 reshape.85
  19.6 0.6 copy.53
  20.2 0.5 reshape.86
  20.7 19.6 %all_to_all.41 = bf16[16,24,544]{2,1,0:T(8,128)(2,1)S(1)} all-to-all(bf16[16,24,544]{2,1,0:T(8,128)(2,1)S(1)} %reshape.86), channel_id=1, replica_groups=mesh['wave'=16,'lev'=2] {'wave'}, dimensions={0} | all-to-all | bytes 835584 | tf_op jit(solution)/shard_map/all_to_all | solution.py:35
  40.3 0.5 reshape.87
  40.8 0.7 fusion.5
  41.5 0.4 copy.55
  41.9 1.3 %reshape.88 = bf16[16,24,544]{2,1,0:T(8,128)(2,1)} reshape(bf16[16,24,4,136]{3,2,1,0:T(4,128)(2,1)S(1)} %copy.55) | data formatting | bytes 835584 | tf_op jit(solution)/shard_map/reshape | solution.py:40
  43.2 4.1 %all-to-all-start.2 = ((bf16[16,24,544]{2,1,0:T(8,128)(2,1)}), bf16[16,24,544]{2,1,0:T(8,128)(2,1)S(1)}, u32[]{:S(2)}, u32[]{:S(2)}) async-start(bf16[16,24,544]{2,1,0:T(8,128)(2,1)} %reshape.88), calls=%async_computation.2 | async-start | bytes 983040 | tf_op jit(solution)/shard_map/all_to_all | solution.py:41
  47.3 0.1 dynamic_slice.3
  47.4 13.6 %all-to-all-done.2 = bf16[16,24,544]{2,1,0:T(8,128)(2,1)S(1)} async-done(((bf16[16,24,544]{2,1,0:T(8,128)(2,1)}), bf16[16,24,544]{2,1,0:T(8,128)(2,1)S(1)}, u32[]{:S(2)}, u32[]{:S(2)}) %all-to-all-start.2) | async-done | bytes 417824 | tf_op jit(solution)/shard_map/all_to_all | solution.py:41
  61.1 0.5 reshape.89
  61.6 0.9 copy.56
  62.5 0.3 fusion.8
  62.8 0.1 pad_maximum_fusion
  62.9 1.2 %copy.57 = bf16[2,4,136,384]{3,1,0,2:T(4,128)(2,1)} copy(bf16[2,4,136,384]{3,2,1,0:T(8,128)(2,1)S(1)} %pad_maximum_fusion) | data formatting | bytes 1671168 | tf_op jit(solution)/shard_map/stack | solution.py:46
  64.1 3.5 %all-to-all-start.3 = ((bf16[2,4,136,384]{3,1,0,2:T(4,128)(2,1)}), bf16[2,4,136,384]{3,1,0,2:T(4,128)(2,1)S(1)}, u32[]{:S(2)}, u32[]{:S(2)}) async-start(bf16[2,4,136,384]{3,1,0,2:T(4,128)(2,1)} %copy.57), calls=%async_computation.3 | async-start | bytes 1671168 | tf_op jit(solution)/shard_map/all_to_all | solution.py:47
  67.7 0.8 add_divide_fusion
  68.5 11.0 %all-to-all-done.3 = bf16[2,4,136,384]{3,1,0,2:T(4,128)(2,1)S(1)} async-done(((bf16[2,4,136,384]{3,1,0,2:T(4,128)(2,1)}), bf16[2,4,136,384]{3,1,0,2:T(4,128)(2,1)S(1)}, u32[]{:S(2)}, u32[]{:S(2)}) %all-to-all-start.3) | async-done | bytes 835616 | tf_op jit(solution)/shard_map/all_to_all | solution.py:47
  79.5 0.3 copy.58
  79.8 1.0 %slice_convert_fusion = (f32[1,4,68,2,384]{4,1,2,3,0:T(4,128)S(1)}, bf16[1,4,68,2,384]{4,1,2,3,0:T(4,128)(2,1)}) fusion(bf16[2,4,68,2,384]{4,1,2,3,0:T(4,128)(2,1)S(1)} %bitcast.35), kind=kLoop, calls=%fused_computation.14 | loop fusion | flops 208896 | bytes 2088960 | tf_op jit(solution)/shard_map/convert_element_type | solution.py:50
  80.8 0.4 copy.61
  81.2 0.7 reshape.90
  81.9 1.3 %copy.59 = bf16[1,4,68,2,384]{4,3,2,1,0:T(2,128)(2,1)S(1)} copy(bf16[1,4,68,2,384]{4,1,2,3,0:T(4,128)(2,1)} %get-tuple-element.16) | data formatting | bytes 835584 | tf_op jit(solution)/shard_map/slice | solution.py:49
  83.2 0.3 squeeze.8
  83.5 1.5 %fusion.11 = (bf16[2,2,68,768]{3,2,1,0:T(8,128)(2,1)S(1)}, bf16[2,2,68,768]{3,2,1,0:T(8,128)(2,1)S(1)}, bf16[2,2,68,768]{3,2,1,0:T(8,128)(2,1)S(1)}) fusion(f32[2,2,68,768]{3,2,1,0:T(8,128)S(1)} %reshape.90, bf16[2,2,68,768]{3,1,2,0:T(2,128)(2,1)} %param.9, pred[2,768]{1,0:T(4,128)(4,1)S(1)} %iota_compare_fusion, bf16[2,2,68,768]{3,2,1,0:T(8,128)(2,1)S(1)} %squeeze.8, ...), kind=kLoop, calls=%fused_computation.12 | loop fusion | flops 1880064 | bytes 3552768 | tf_op jit(solution)/shard_map/jit(_where)/select_n | solution.py:62
  85.1 1.1 %copy.64 = bf16[2,2,68,768]{3,1,2,0:T(2,128)(2,1)} copy(bf16[2,2,68,768]{3,2,1,0:T(8,128)(2,1)S(1)} %get-tuple-element.17) | data formatting | bytes 835584
  86.1 1.1 %copy.63 = bf16[2,2,68,768]{3,1,2,0:T(2,128)(2,1)} copy(bf16[2,2,68,768]{3,2,1,0:T(8,128)(2,1)S(1)} %get-tuple-element.18) | data formatting | bytes 835584
  87.2 1.1 %copy.62 = bf16[2,2,68,768]{3,1,2,0:T(2,128)(2,1)} copy(bf16[2,2,68,768]{3,2,1,0:T(8,128)(2,1)S(1)} %get-tuple-element.19) | data formatting | bytes 835584
  (10 shorter events, 0.1 us)
Async XLA Ops:
  0.6 40.2 %copy-start = (bf16[1,24,136,136]{3,2,1,0:T(8,128)(2,1)S(1)}, bf16[1,24,136,136]{3,2,1,0:T(8,128)(2,1)}, u32[]{:S(2)}) copy-start(bf16[1,24,136,136]{3,2,1,0:T(8,128)(2,1)} %param.10) | copy-start | bytes 2663428
  41.5 5.8 %copy-start.3 = (f32[136]{0:T(256)S(1)}, f32[136]{0:T(256)}, u32[]{:S(2)}) copy-start(f32[136]{0:T(256)} %param.12) | copy-start | bytes 1636
  43.2 19.3 %copy-start.1 = (bf16[136,136]{1,0:T(8,128)(2,1)S(1)}, bf16[136,136]{1,0:T(8,128)(2,1)}, u32[]{:S(2)}) copy-start(bf16[136,136]{1,0:T(8,128)(2,1)} %param.11) | copy-start | bytes 110980
  43.2 17.9 %all-to-all-start.2 = ((bf16[16,24,544]{2,1,0:T(8,128)(2,1)}), bf16[16,24,544]{2,1,0:T(8,128)(2,1)S(1)}, u32[]{:S(2)}, u32[]{:S(2)}) async-start(bf16[16,24,544]{2,1,0:T(8,128)(2,1)} %reshape.88), calls=%async_computation.2 | async-start | bytes 983040 | tf_op jit(solution)/shard_map/all_to_all | solution.py:41
  62.9 4.8 %copy-start.2 = (s32[2]{0:T(128)S(1)}, s32[2]{0:T(128)}, u32[]{:S(2)}) copy-start(s32[2]{0:T(128)} %param.13) | copy-start | bytes 28
  64.1 15.4 %all-to-all-start.3 = ((bf16[2,4,136,384]{3,1,0,2:T(4,128)(2,1)}), bf16[2,4,136,384]{3,1,0,2:T(4,128)(2,1)S(1)}, u32[]{:S(2)}, u32[]{:S(2)}) async-start(bf16[2,4,136,384]{3,1,0,2:T(4,128)(2,1)} %copy.57), calls=%async_computation.3 | async-start | bytes 1671168 | tf_op jit(solution)/shard_map/all_to_all | solution.py:47
where the time goes:
time: 88.8 us; the launch traced here: 88.3 us
  blocking collectives  34.4 us (39%)
  waiting for transfers between devices  24.6 us (28%)
  local copies, waits for them, and re-layouts  16.3 us (18%)
  starting transfers between devices  7.66 us (9%)
  other arithmetic  3.5 us (4%)
  matrix products  0.91 us (1%)
    all_to_all x1, blocking collectives, on_device(): lax.all_to_all(outgoing, 'wave', split_axis=0, concat_axis=0, tiled=True)  19.6 us
    all_to_all x1, blocking collectives, on_device(): lax.all_to_all(spreading_source, 'lev', split_axis=3, concat_axis=2, tile...  14.8 us
    all_to_all x1, waiting for transfers between devices, on_device(): lax.all_to_all(solved_columns, 'wave', split_axis=0, concat_axis=0, tiled...  13.6 us
    all_to_all x1, waiting for transfers between devices, on_device(): both = lax.all_to_all(both, 'lev', split_axis=2, concat_axis=3, tiled=True)  11 us
    unnamed x12, local copies, waits for them, and re-layouts  6.1 us
    all_to_all x1, starting transfers between devices, on_device(): lax.all_to_all(solved_columns, 'wave', split_axis=0, concat_axis=0, tiled...  4.12 us
    all_to_all x1, starting transfers between devices, on_device(): both = lax.all_to_all(both, 'lev', split_axis=2, concat_axis=3, tiled=True)  3.54 us
  transfers between devices with their start and end apart: 2, of which 2 were waited for; matrix products, arithmetic and copies ran while one was open for 1% of the time, Pallas kernels for 0%

commit v1 on v0

--- a/solution.py
+++ b/solution.py
@@ -29,7 +29,16 @@
     empty_placeholder = jnp.zeros((), jnp.bfloat16)
     wave_count = lax.axis_size("wave")
     local_n = block_n // wave_count
-    rhs_div = lax.all_to_all(spreading_source, "lev", split_axis=3, concat_axis=2, tiled=True)
+
+    def _feed_skins(q_in, a_name):
+        carry = lax.psum(1, a_name)
+        field_out = jnp.split(q_in, carry, axis=3)
+        heard = jnp.stack(field_out)
+        opened = lax.all_to_all(heard, a_name, 0, 0)
+        block_last = jnp.concatenate(opened, axis=2)
+        return block_last
+
+    rhs_div = _feed_skins(spreading_source, "lev")
     outgoing = rhs_div.reshape(flat_rows, layer_count, wave_count, local_n).transpose(2, 3, 0, 1)
     outgoing = outgoing.reshape(wave_count, local_n, flat_rows * layer_count)
     columns = lax.all_to_all(outgoing, "wave", split_axis=0, concat_axis=0, tiled=True)

time: 88.8 us -> 84.4 us (0.950)
  blocking collectives: 34.4 us -> 30.4 us
  local copies, waits for them, and re-layouts: 16.3 us -> 15.3 us
    all_to_all x1, blocking collectives: 14.8 us -> 10.9 us  [_feed_skins(): opened = lax.all_to_all(heard, a_name, 0, 0)]
    unnamed x12 -> x11, local copies, waits for them, and re-layouts: 6.1 us -> 3.25 us
    another operation x0 -> x2, local copies, waits for them, and re-layouts: none -> 1.89 us  [the longest x1 1.44 us: _feed_skins(): heard = jnp.stack(field_out)]
where the time goes in v1:
time: 84.4 us; the launch traced here: 83.9 us
  blocking collectives  30.4 us (36%)
  waiting for transfers between devices  24.6 us (29%)
  local copies, waits for them, and re-layouts  15.3 us (18%)
  starting transfers between devices  7.66 us (9%)
  other arithmetic  4.09 us (5%)
  matrix products  0.91 us (1%)
    all_to_all x1, blocking collectives, on_device(): lax.all_to_all(outgoing, 'wave', split_axis=0, concat_axis=0, tiled=True)  19.5 us
    all_to_all x1, waiting for transfers between devices, on_device(): lax.all_to_all(solved_columns, 'wave', split_axis=0, concat_axis=0, tiled...  13.6 us
    all_to_all x1, waiting for transfers between devices, on_device(): both = lax.all_to_all(both, 'lev', split_axis=2, concat_axis=3, tiled=True)  11 us
    all_to_all x1, blocking collectives, _feed_skins(): opened = lax.all_to_all(heard, a_name, 0, 0)  10.9 us
    all_to_all x1, starting transfers between devices, on_device(): lax.all_to_all(solved_columns, 'wave', split_axis=0, concat_axis=0, tiled...  4.12 us
    all_to_all x1, starting transfers between devices, on_device(): both = lax.all_to_all(both, 'lev', split_axis=2, concat_axis=3, tiled=True)  3.54 us
    unnamed x11, local copies, waits for them, and re-layouts  3.25 us
  transfers between devices with their start and end apart: 2, of which 2 were waited for; matrix products, arithmetic and copies ran while one was open for 1% of the time, Pallas kernels for 0%

profile of v1, /device:TPU:0, one launch (start us, length us, event | category | flops | bytes accessed | tf_op | source)
XLA Modules:
  0.0 83.9 jit_solution(10235607830883177280)
XLA Ops:
  0.6 1.4 %slice_bitcast_fusion.1 = (bf16[1,2,2,68,384]{4,2,3,1,0:T(2,128)(2,1)S(1)}, bf16[1,2,2,68,384]{4,2,3,1,0:T(2,128)(2,1)S(1)}) fusion(bf16[2,2,68,768]{3,1,2,0:T(2,128)(2,1)} %param.8), kind=kLoop, calls=%fused_computation.18 | loop fusion | bytes 835584 | tf_op jit(solution)/shard_map/stack | solution.py:36
  2.1 0.6 pad_maximum_fusion.1
  2.7 10.9 %all_to_all.30 = bf16[2,2,2,68,384]{4,2,3,1,0:T(2,128)(2,1)S(1)} all-to-all(bf16[2,2,2,68,384]{4,2,3,1,0:T(2,128)(2,1)S(1)} %pad_maximum_fusion.1), channel_id=1, replica_groups=mesh['wave'=16,'lev'=2] {'lev'}, dimensions={0} | all-to-all | bytes 835584 | tf_op jit(solution)/shard_map/all_to_all | solution.py:37
  13.6 1.2 %copy.36 = bf16[2,2,2,68,384]{3,2,4,1,0:T(2,128)(2,1)S(1)} copy(bf16[2,2,2,68,384]{4,1,3,0,2:T(2,128)(2,1)S(1)} %bitcast.38) | data formatting | bytes 835584 | tf_op jit(solution)/shard_map/reshape | solution.py:38
  14.8 0.4 reshape_reshape.3
  15.2 0.6 copy.37
  15.9 0.5 reshape.85
  16.4 19.5 %all_to_all.31 = bf16[16,24,544]{2,1,0:T(8,128)(2,1)S(1)} all-to-all(bf16[16,24,544]{2,1,0:T(8,128)(2,1)S(1)} %reshape.85), channel_id=1, replica_groups=mesh['wave'=16,'lev'=2] {'wave'}, dimensions={0} | all-to-all | bytes 835584 | tf_op jit(solution)/shard_map/all_to_all | solution.py:44
  35.9 0.5 reshape.86
  36.4 0.7 fusion.5
  37.1 0.4 copy.39
  37.5 1.3 %reshape.87 = bf16[16,24,544]{2,1,0:T(8,128)(2,1)} reshape(bf16[16,24,4,136]{3,2,1,0:T(4,128)(2,1)S(1)} %copy.39) | data formatting | bytes 835584 | tf_op jit(solution)/shard_map/reshape | solution.py:49
  38.8 4.1 %all-to-all-start.2 = ((bf16[16,24,544]{2,1,0:T(8,128)(2,1)}), bf16[16,24,544]{2,1,0:T(8,128)(2,1)S(1)}, u32[]{:S(2)}, u32[]{:S(2)}) async-start(bf16[16,24,544]{2,1,0:T(8,128)(2,1)} %reshape.87), calls=%async_computation.2 | async-start | bytes 983040 | tf_op jit(solution)/shard_map/all_to_all | solution.py:50
  43.0 13.6 %all-to-all-done.2 = bf16[16,24,544]{2,1,0:T(8,128)(2,1)S(1)} async-done(((bf16[16,24,544]{2,1,0:T(8,128)(2,1)}), bf16[16,24,544]{2,1,0:T(8,128)(2,1)S(1)}, u32[]{:S(2)}, u32[]{:S(2)}) %all-to-all-start.2) | async-done | bytes 417824 | tf_op jit(solution)/shard_map/all_to_all | solution.py:50
  56.7 0.5 reshape.88
  57.2 0.9 %copy.40 = bf16[384,4,136]{0,2,1:T(8,128)(2,1)S(1)} copy(bf16[384,4,136]{2,1,0:T(4,128)(2,1)S(1)} %reshape.88) | data formatting | bytes 835584 | tf_op jit(solution)/shard_map/reshape | solution.py:51
  58.1 0.3 fusion.8
  58.3 0.1 pad_maximum_fusion
  58.5 1.2 %copy.41 = bf16[2,4,136,384]{3,1,0,2:T(4,128)(2,1)} copy(bf16[2,4,136,384]{3,2,1,0:T(8,128)(2,1)S(1)} %pad_maximum_fusion) | data formatting | bytes 1671168 | tf_op jit(solution)/shard_map/stack | solution.py:55
  59.7 3.5 %all-to-all-start.3 = ((bf16[2,4,136,384]{3,1,0,2:T(4,128)(2,1)}), bf16[2,4,136,384]{3,1,0,2:T(4,128)(2,1)S(1)}, u32[]{:S(2)}, u32[]{:S(2)}) async-start(bf16[2,4,136,384]{3,1,0,2:T(4,128)(2,1)} %copy.41), calls=%async_computation.3 | async-start | bytes 1671168 | tf_op jit(solution)/shard_map/all_to_all | solution.py:56
  63.3 0.8 add_divide_fusion
  64.1 11.0 %all-to-all-done.3 = bf16[2,4,136,384]{3,1,0,2:T(4,128)(2,1)S(1)} async-done(((bf16[2,4,136,384]{3,1,0,2:T(4,128)(2,1)}), bf16[2,4,136,384]{3,1,0,2:T(4,128)(2,1)S(1)}, u32[]{:S(2)}, u32[]{:S(2)}) %all-to-all-start.3) | async-done | bytes 835616 | tf_op jit(solution)/shard_map/all_to_all | solution.py:56
  75.1 0.3 copy.42
  75.4 1.0 %slice_convert_fusion = (f32[1,4,68,2,384]{4,1,2,3,0:T(4,128)S(1)}, bf16[1,4,68,2,384]{4,1,2,3,0:T(4,128)(2,1)}) fusion(bf16[2,4,68,2,384]{4,1,2,3,0:T(4,128)(2,1)S(1)} %bitcast.36), kind=kLoop, calls=%fused_computation.13 | loop fusion | flops 208896 | bytes 2088960 | tf_op jit(solution)/shard_map/convert_element_type | solution.py:59
  76.4 0.4 copy.45
  76.8 0.7 reshape.89
  77.5 1.3 %copy.43 = bf16[1,4,68,2,384]{4,3,2,1,0:T(2,128)(2,1)S(1)} copy(bf16[1,4,68,2,384]{4,1,2,3,0:T(4,128)(2,1)} %get-tuple-element.13) | data formatting | bytes 835584 | tf_op jit(solution)/shard_map/slice | solution.py:58
  78.8 0.3 squeeze.8
  79.1 1.5 %fusion.11 = (bf16[2,2,68,768]{3,2,1,0:T(8,128)(2,1)S(1)}, bf16[2,2,68,768]{3,2,1,0:T(8,128)(2,1)S(1)}, bf16[2,2,68,768]{3,2,1,0:T(8,128)(2,1)S(1)}) fusion(f32[2,2,68,768]{3,2,1,0:T(8,128)S(1)} %reshape.89, bf16[2,2,68,768]{3,1,2,0:T(2,128)(2,1)} %param.9, pred[2,768]{1,0:T(4,128)(4,1)S(1)} %iota_compare_fusion, bf16[2,2,68,768]{3,2,1,0:T(8,128)(2,1)S(1)} %squeeze.8, ...), kind=kLoop, calls=%fused_computation.11 | loop fusion | flops 1880064 | bytes 3552768 | tf_op jit(solution)/shard_map/jit(_where)/select_n | solution.py:71
  80.6 1.1 %copy.48 = bf16[2,2,68,768]{3,1,2,0:T(2,128)(2,1)} copy(bf16[2,2,68,768]{3,2,1,0:T(8,128)(2,1)S(1)} %get-tuple-element.16) | data formatting | bytes 835584
  81.7 1.1 %copy.47 = bf16[2,2,68,768]{3,1,2,0:T(2,128)(2,1)} copy(bf16[2,2,68,768]{3,2,1,0:T(8,128)(2,1)S(1)} %get-tuple-element.17) | data formatting | bytes 835584
  82.8 1.1 %copy.46 = bf16[2,2,68,768]{3,1,2,0:T(2,128)(2,1)} copy(bf16[2,2,68,768]{3,2,1,0:T(8,128)(2,1)S(1)} %get-tuple-element.18) | data formatting | bytes 835584
  (11 shorter events, 0.2 us)
Async XLA Ops:
  0.6 35.8 %copy-start = (bf16[1,24,136,136]{3,2,1,0:T(8,128)(2,1)S(1)}, bf16[1,24,136,136]{3,2,1,0:T(8,128)(2,1)}, u32[]{:S(2)}) copy-start(bf16[1,24,136,136]{3,2,1,0:T(8,128)(2,1)} %param.10) | copy-start | bytes 2663428
  37.1 5.9 %copy-start.3 = (f32[136]{0:T(256)S(1)}, f32[136]{0:T(256)}, u32[]{:S(2)}) copy-start(f32[136]{0:T(256)} %param.12) | copy-start | bytes 1636
  38.8 19.3 %copy-start.1 = (bf16[136,136]{1,0:T(8,128)(2,1)S(1)}, bf16[136,136]{1,0:T(8,128)(2,1)}, u32[]{:S(2)}) copy-start(bf16[136,136]{1,0:T(8,128)(2,1)} %param.11) | copy-start | bytes 110980
  38.8 17.9 %all-to-all-start.2 = ((bf16[16,24,544]{2,1,0:T(8,128)(2,1)}), bf16[16,24,544]{2,1,0:T(8,128)(2,1)S(1)}, u32[]{:S(2)}, u32[]{:S(2)}) async-start(bf16[16,24,544]{2,1,0:T(8,128)(2,1)} %reshape.87), calls=%async_computation.2 | async-start | bytes 983040 | tf_op jit(solution)/shard_map/all_to_all | solution.py:50
  58.4 4.8 %copy-start.2 = (s32[2]{0:T(128)S(1)}, s32[2]{0:T(128)}, u32[]{:S(2)}) copy-start(s32[2]{0:T(128)} %param.13) | copy-start | bytes 28
  59.7 15.4 %all-to-all-start.3 = ((bf16[2,4,136,384]{3,1,0,2:T(4,128)(2,1)}), bf16[2,4,136,384]{3,1,0,2:T(4,128)(2,1)S(1)}, u32[]{:S(2)}, u32[]{:S(2)}) async-start(bf16[2,4,136,384]{3,1,0,2:T(4,128)(2,1)} %copy.41), calls=%async_computation.3 | async-start | bytes 1671168 | tf_op jit(solution)/shard_map/all_to_all | solution.py:56
